TPU v7x, 32 devices: a whole 2x2x4 slice. The times are simulated.
32 devices in a mesh: parts: 2 (over y), space: 4 (over z), tm: 2 (over x), spin: 2 (over core).
Axes of the slice: x: 2, y: 2, z: 4, core: 2. Of those that a mesh axis runs over, the one named last changes fastest.
Arguments:
- backward: bfloat16 [4, 2, 4, 64, 3, 4, 128], P('parts', 'tm', None, 'spin', None, 'space'), parts along dimension 0, may hold values from -6 to 6
- forward: bfloat16 [4, 2, 4, 64, 3, 4, 128], P('parts', 'tm', None, 'spin', None, 'space'), parts along dimension 0, may hold values from -6 to 6
- gauge_links: bfloat16 [4, 3, 3, 3, 2, 4, 128], P('parts', None, None, None, 'tm', 'space'), parts along dimension 0, may hold values from -2.5 to 2.5
- momenta: int32 [3, 3], replicated, may hold values from -2 to 2
- gamma_list: int32 [16], replicated, may hold values from 0 to 15
Outputs:
- insertion: float32 [4, 3, 16, 2, 64, 64], P('parts', None, None, 'tm', 'space', 'spin'), parts along dimension 0
There are 2 independent parts, one for each index of `parts`. A program takes and returns all parts, laid end to end along the dimension named above; an argument that names none is the same for every part. Nothing has to cross between parts.
All inputs are finite; a program needn't handle non-finite values.
Results may differ from a plain program's by a relative error of at most 0.0056.
Values may be sent and summed in bfloat16 or wider, within the bound.
No kernel may reach another device: no remote copies, remote signals or barrier semaphores. Data moves between devices by JAX's collectives and lax.ppermute only.
A program may use at most 64 MiB of HBM per device.

v0:
```python
import functools
import math

import jax
import jax.numpy as jnp
import numpy as np
from jax import lax
from jax.experimental import pallas as pl
from jax.experimental.pallas import tpu as pltpu
from jax.sharding import PartitionSpec as P


LX = 32
F32 = jnp.float32
BF16 = jnp.bfloat16
VMEM = pl.BlockSpec(memory_space=pltpu.VMEM)
HBM = pl.BlockSpec(memory_space=pltpu.HBM)


def gamma_tables():
    zeros = np.zeros((4, 4))
    gx_imag = np.array([[0, 0, 0, 1], [0, 0, 1, 0], [0, -1, 0, 0], [-1, 0, 0, 0]]) * 1.0
    gy_real = np.array([[0, 0, 0, -1], [0, 0, 1, 0], [0, 1, 0, 0], [-1, 0, 0, 0]]) * 1.0
    gz_imag = np.array([[0, 0, 1, 0], [0, 0, 0, -1], [-1, 0, 0, 0], [0, 1, 0, 0]]) * 1.0
    gt_real = np.array([[0, 0, 1, 0], [0, 0, 0, 1], [1, 0, 0, 0], [0, 1, 0, 0]]) * 1.0
    singles = [zeros + 1j * gx_imag, gy_real + 0j, zeros + 1j * gz_imag, gt_real + 0j]
    basis = []
    for number in range(16):
        matrix = np.eye(4) + 0j
        for which in range(4):
            if number >> which & 1:
                matrix = matrix @ singles[which]
        basis.append(matrix)
    return (singles, basis)


SINGLES, BASIS = gamma_tables()


def unit_rows(matrix):
    columns = [int(np.flatnonzero(row)[0]) for row in matrix]
    return (columns, [complex(matrix[r, c]) for r, c in enumerate(columns)])


def plus_unit(total, unit, value):
    total_real, total_imag = total
    real, imag = value
    if unit == 1:
        return (total_real + real, total_imag + imag)
    if unit == -1:
        return (total_real - real, total_imag - imag)
    if unit == 1j:
        return (total_real - imag, total_imag + real)
    return (total_real + imag, total_imag - real)


def half_spinor(spinor, direction, sign):
    columns, units = unit_rows(SINGLES[direction])
    return [
        [plus_unit(spinor(s, c), sign * units[s], spinor(columns[s], c)) for c in range(3)]
        for s in range(2)
    ]


def colour_product(link, half, dagger):
    result = []
    for colours in half:
        row = []
        for c in range(3):
            real = imag = None
            for d in range(3):
                u_real, u_imag = link(d, c) if dagger else link(c, d)
                h_real, h_imag = colours[d]
                if dagger:
                    part_real = u_real * h_real + u_imag * h_imag
                    part_imag = u_real * h_imag - u_imag * h_real
                else:
                    part_real = u_real * h_real - u_imag * h_imag
                    part_imag = u_real * h_imag + u_imag * h_real
                real = part_real if real is None else real + part_real
                imag = part_imag if imag is None else imag + part_imag
            row.append((real, imag))
        result.append(row)
    return result


def add_hop(total, half, direction, sign, weight):
    columns, units = unit_rows(SINGLES[direction])
    for c in range(3):
        for s in range(2):
            total[s][c] = plus_unit(total[s][c], weight, half[s][c])
        for s in range(2, 4):
            total[s][c] = plus_unit(total[s][c], weight * sign * units[s], half[columns[s]][c])


def shifted(value, offset, along_y, width):
    plane = value.shape[-1]
    if along_y:
        return pltpu.roll(value, -offset * width % plane, 1)
    lane = lax.broadcasted_iota(jnp.int32, value.shape, 1) % width
    edge = width - 1 if offset == 1 else 0
    near = pltpu.roll(value, -offset % plane, 1)
    far = pltpu.roll(value, offset * (width - 1) % plane, 1)
    return jnp.where(lane == edge, far, near)


def part(real_imag, s, c):
    return (real_imag * 4 + s) * 3 + c


def half_part(real_imag, s, c):
    return (real_imag * 2 + s) * 3 + c


def link_reader(links_ref, direction):
    def link(row, column):
        pair = links_ref[(direction * 3 + row) * 3 + column].astype(F32)
        return (pair[0:1], pair[1:2])

    return link


def spinor_reader(ref, rows):
    def spinor(s, c):
        return (ref[part(0, s, c), rows].astype(F32), ref[part(1, s, c), rows].astype(F32))

    return spinor


def over_rows(count, step, body):
    def stage(number, carry):
        body(pl.ds(pl.multiple_of(number * step, step), step))
        return carry

    lax.fori_loop(0, count // step, stage, 0)


def copy_all(pairs, sems):
    copies = [pltpu.make_async_copy(*pair, sems.at[i]) for i, pair in enumerate(pairs)]
    for copy in copies:
        copy.start()
    return copies


def halo_kernel(fwd_hbm, links_hbm, up_ref, down_ref, fwd_ref, links_ref, sems):
    for copy in copy_all(((fwd_hbm, fwd_ref), (links_hbm, links_ref)), sems):
        copy.wait()
    link = link_reader(links_ref, 2)

    def rows_body(rows):
        spinor = spinor_reader(fwd_ref, rows)
        ahead = half_spinor(spinor, 2, -1)
        behind = colour_product(link, half_spinor(spinor, 2, 1), True)
        for s in range(2):
            for c in range(3):
                for ri in range(2):
                    place = half_part(ri, s, c)
                    up_ref[place, rows] = ahead[s][c][ri].astype(BF16)
                    down_ref[place, rows] = behind[s][c][ri].astype(BF16)

    over_rows(fwd_ref.shape[1], 16, rows_body)


def table_place(number):
    x = (number ^ (number >> 1)) & 1
    y = ((number >> 2) ^ (number >> 3)) & 1
    q = (number & 1) | ((number >> 2) & 1) << 1
    return 4 * q + ((3 * x) ^ (2 * y))


def local_kernel(
    momenta_hbm, own_hbm, list_hbm, fwd_ref, links_ref, other_ref,
    weave_ref, left_ref, places_ref, phase_ref, momenta_ref, own_ref, list_ref, sems,
    *, width, spaces, ordered,
):
    copies = copy_all(
        ((momenta_hbm, momenta_ref), (own_hbm, own_ref), (list_hbm, list_ref)), sems
    )
    columns, plane = fwd_ref.shape[1:]
    z_place = lax.axis_index("space")
    core = lax.axis_index("spin")

    def rows_body(rows):
        spinor = spinor_reader(fwd_ref, rows)
        total = [[(0.0, 0.0) for _ in range(3)] for _ in range(4)]
        for direction in range(2):
            link = link_reader(links_ref, direction)
            along_y = direction == 1
            half = half_spinor(spinor, direction, -1)
            half = [[tuple(shifted(v, 1, along_y, width) for v in z) for z in row] for row in half]
            add_hop(total, colour_product(link, half, False), direction, -1, 1)
            half = colour_product(link, half_spinor(spinor, direction, 1), True)
            half = [[tuple(shifted(v, -1, along_y, width) for v in z) for z in row] for row in half]
            add_hop(total, half, direction, 1, -1)
        for s in range(4):
            for c in range(3):
                for ri in range(2):
                    weave_ref[part(ri, s, c), rows] = total[s][c][ri]

    over_rows(columns, 8, rows_body)

    def whole_mod(value, modulus):
        return value - modulus * jnp.floor((value + 0.5) / modulus)

    site = lax.broadcasted_iota(jnp.int32, (1, plane), 1).astype(F32)
    row_of = jnp.floor((site + 0.5) / width)
    x_of = site - width * row_of
    height = plane // width
    for copy in copies:
        copy.wait()
    for p in range(phase_ref.shape[0]):
        mom = [momenta_ref[p, axis].astype(F32) for axis in range(3)]
        frac = whole_mod(mom[0] * x_of, width) / width + whole_mod(mom[1] * row_of, height) / height
        depth = jnp.full((1, plane), mom[2] * z_place.astype(F32), F32)
        theta = 2.0 * math.pi * (whole_mod(depth, spaces) / spaces + frac)
        phase_ref[p, 0:1] = jnp.cos(theta)
        phase_ref[p, 1:2] = jnp.sin(theta)

    for k in range(list_ref.shape[0]):
        places_ref[pl.ds(k, 1)] = jnp.full((1, places_ref.shape[1]), table_place(list_ref[k]))

    moms = phase_ref.shape[0]
    block = 2 * columns // spaces if ordered else columns

    def rotate(spinor, first, mom_step, spin_step):
        for p in range(moms):
            cosine = phase_ref[p, 0:1]
            sine = phase_ref[p, 1:2]
            for s in range(4):
                at = pl.ds(pl.multiple_of(first + p * mom_step + s * spin_step, block), block)
                for c in range(3):
                    real, imag = spinor(s, c)
                    lanes = pl.ds(c * plane, plane)
                    left_ref[at, lanes] = (cosine * real - sine * imag).astype(BF16)
                    lanes = pl.ds((3 + c) * plane, plane)
                    left_ref[at, lanes] = (sine * real + cosine * imag).astype(BF16)

    for source_ref, half in ((own_ref, core), (other_ref, 1 - core)):
        for number in range(columns // block):
            spinor = spinor_reader(source_ref, pl.ds(number * block, block))
            if ordered:
                k = (half * (columns // block) + number - z_place + spaces) % spaces
                rotate(spinor, k * moms * 4 * block, 4 * block, block)
            else:
                rotate(spinor, half * columns, 8 * columns, 2 * columns)


def multiply(left_ref, right_ref, outs, first_block, moms):
    height = outs[0].shape[0]
    wide = right_ref.shape[0]
    share = moms * height
    pairs = lax.dot_general(
        left_ref[pl.ds(first_block * share, len(outs) * share)],
        right_ref[...],
        (((1,), (1,)), ((), ())),
        preferred_element_type=F32,
    )
    for number, out_ref in enumerate(outs):
        for p in range(moms):
            first = number * share + p * height
            out_ref[:, pl.ds(p * wide, wide)] = pairs[first : first + height].astype(out_ref.dtype)


def first_pairs_kernel(
    weave_ref, ahead_ref, behind_ref, links_ref, left_ref, right_ref, out_ref, *, first_block, moms
):
    columns, plane = weave_ref.shape[1:]
    wide = 4 * columns
    link = link_reader(links_ref, 2)

    def half_reader(ref, rows):
        return [
            [tuple(ref[half_part(ri, s, c), rows].astype(F32) for ri in range(2)) for c in range(3)]
            for s in range(2)
        ]

    def rows_body(rows):
        total = [
            [(weave_ref[part(0, s, c), rows], weave_ref[part(1, s, c), rows]) for c in range(3)]
            for s in range(4)
        ]
        add_hop(total, colour_product(link, half_reader(ahead_ref, rows), False), 2, -1, 1)
        add_hop(total, half_reader(behind_ref, rows), 2, 1, -1)
        for s in range(4):
            at_real = pl.ds(pl.multiple_of(s * columns + rows.start, 8), rows.size)
            at_imag = pl.ds(pl.multiple_of(wide + s * columns + rows.start, 8), rows.size)
            for c in range(3):
                real, imag = total[s][c]
                first = pl.ds(c * plane, plane)
                second = pl.ds((3 + c) * plane, plane)
                right_ref[at_real, first] = real.astype(BF16)
                right_ref[at_real, second] = imag.astype(BF16)
                right_ref[at_imag, first] = imag.astype(BF16)
                right_ref[at_imag, second] = (-real).astype(BF16)

    over_rows(columns, 8, rows_body)
    multiply(left_ref, right_ref, [out_ref], first_block, moms)


def other_pairs_kernel(left_ref, right_ref, own_ref, *out_refs, moms):
    multiply(left_ref, right_ref, [own_ref], 0, moms)
    if out_refs:
        multiply(left_ref, right_ref, out_refs, 2, moms)


def insertion_kernel(places_ref, *rest, scaling):
    *in_refs, out_hbm, table_ref, out_ref, sems = rest
    moms, _, count, block, columns = out_ref.shape
    wide = 4 * columns
    group = lax.broadcasted_iota(jnp.int32, (1, wide), 1) // columns

    def by_group(values):
        result = jnp.full((1, wide), values[0], F32)
        for j in range(1, 4):
            result = jnp.where(group == j, values[j], result)
        return result

    weights = []
    for q in range(4):
        rows = []
        for s in range(4):
            units = []
            for j in range(4):
                x, y = {0: (0, 0), 3: (1, 0), 2: (0, 1), 1: (1, 1)}[j]
                first, third = q & 1, q >> 1
                number = first | (first ^ x) << 1 | third << 2 | (third ^ y) << 3
                units.append(complex(BASIS[number][s, s ^ j]) * scaling)
            rows.append((by_group([u.real for u in units]), by_group([u.imag for u in units])))
        weights.append(rows)

    even = group % 2 == 0

    def crossed(value, s):
        if s & 1:
            value = jnp.where(
                even, pltpu.roll(value, wide - columns, 1), pltpu.roll(value, columns, 1)
            )
        if s & 2:
            value = pltpu.roll(value, 2 * columns, 1)
        return value

    places = [places_ref[pl.ds(k, 1), pl.ds(0, 1)][0, 0] for k in range(count)]

    def one_momentum(p):
        spins = []
        for s in range(4):
            both = []
            for ri in range(2):
                lanes = pl.ds((2 * p + ri) * wide, wide)
                total = None
                for ref in in_refs:
                    for lead in range(ref.shape[0]):
                        term = ref[lead, pl.ds(s * block, block), lanes].astype(F32)
                        total = term if total is None else total + term
                both.append(crossed(total, s))
            spins.append(both)
        for q in range(4):
            real = imag = None
            for s in range(4):
                w_real, w_imag = weights[q][s]
                a, b = spins[s]
                part_real = w_real * a - w_imag * b
                part_imag = w_real * b + w_imag * a
                real = part_real if real is None else real + part_real
                imag = part_imag if imag is None else imag + part_imag
            for j in range(4):
                for ri, value in enumerate((real, imag)):
                    if j:
                        value = pltpu.roll(value, wide - j * columns, 1)
                    table_ref[p, 4 * q + j, ri] = value[:, :columns]
        for k in range(count):
            for ri in range(2):
                out_ref[p, ri, k] = table_ref[p, places[k], ri]
        output_copy(p).start()

    def output_copy(p):
        return pltpu.make_async_copy(out_ref.at[p], out_hbm.at[:, p], sems.at[p])

    for p in range(moms):
        one_momentum(p)
    for p in range(moms):
        output_copy(p).wait()


def passed_along(value, axis, steps):
    count = lax.axis_size(axis)
    pairs = [(source, (source + steps) % count) for source in range(count)]
    return lax.ppermute(value, axis, pairs)


def call(kernel, out_shape, ins, cost, outs=VMEM, **kwargs):
    many = isinstance(out_shape, (list, tuple))
    return pl.pallas_call(
        kernel,
        out_shape=out_shape,
        in_specs=ins,
        out_specs=[outs] * len(out_shape) if many else outs,
        compiler_params=pltpu.CompilerParams(vmem_limit_bytes=16 * 2**20),
        cost_estimate=pl.CostEstimate(flops=cost, bytes_accessed=2**20, transcendentals=0),
        **kwargs,
    )


def in_hbm(value):
    return pltpu.with_memory_space_constraint(value, pltpu.HBM)


def shape(dims, dtype):
    return jax.ShapeDtypeStruct(dims, dtype)


def body(backward, forward, gauge_links, momenta, gamma_list):
    _, times, _, columns, _, layers, plane = forward.shape
    assert times == 1 and layers == 1
    spaces = lax.axis_size("space")
    moms = momenta.shape[0]
    count = gamma_list.shape[0]
    block = 2 * columns // spaces
    ordered = block % 16 == 0
    fwd = jnp.transpose(forward, (0, 1, 2, 4, 5, 3, 6)).reshape(24, columns, plane)
    own = jnp.transpose(backward, (0, 1, 2, 4, 5, 3, 6)).reshape(24, columns, plane)
    links = jnp.transpose(gauge_links, (1, 2, 3, 4, 5, 0, 6)).reshape(27, 2, plane)

    other = passed_along(own, "spin", 1)
    half = shape((12, columns, plane), BF16)
    to_up, to_down, fwd_here, links_here = call(
        halo_kernel,
        [half, half] + [shape(v.shape, v.dtype) for v in (fwd, links)],
        [HBM] * 2,
        10**7,
        scratch_shapes=[pltpu.SemaphoreType.DMA((2,))],
    )(*[in_hbm(v) for v in (fwd, links)])
    behind = passed_along(to_down, "space", 1)
    ahead = passed_along(to_up, "space", -1)
    rows = 8 * columns
    weave, left, places = call(
        functools.partial(local_kernel, width=LX, spaces=spaces, ordered=ordered),
        [
            shape((24, columns, plane), F32),
            shape((moms * rows, 6 * plane), BF16),
            shape((count, plane), jnp.int32),
        ],
        [HBM, HBM, HBM, VMEM, VMEM, VMEM],
        10**8,
        scratch_shapes=[
            pltpu.VMEM((moms, 2, plane), F32),
            pltpu.SMEM(momenta.shape, jnp.int32),
            pltpu.VMEM(own.shape, BF16),
            pltpu.SMEM(gamma_list.shape, jnp.int32),
            pltpu.SemaphoreType.DMA((3,)),
        ],
    )(in_hbm(momenta), in_hbm(own), in_hbm(gamma_list), fwd_here, links_here, other)
    wide = 8 * columns
    share = rows // spaces if ordered else rows
    pair_shape = shape((share, moms * wide), BF16)
    right, first = call(
        functools.partial(first_pairs_kernel, first_block=int(ordered), moms=moms),
        [shape((wide, 6 * plane), BF16), pair_shape],
        [VMEM] * 5,
        10**9,
    )(weave, ahead, behind, links_here, left)
    if ordered:
        own_pairs, *others = call(
            functools.partial(other_pairs_kernel, moms=moms),
            [shape(pair_shape.shape, F32)] + [pair_shape] * (spaces - 2),
            [VMEM] * 2,
            10**9,
        )(left, right)
        blocks = [own_pairs]
        for k, value in enumerate([first, *others], 1):
            blocks.append(passed_along(value, "space", k))
        blocks = [b[None] for b in blocks]
    else:
        split = first.reshape(4, spaces, block, moms * wide)
        split = jnp.swapaxes(split, 0, 1).reshape(spaces, 4 * block, moms * wide)
        blocks = [lax.all_to_all(split, "space", 0, 0, tiled=True)]
    scaling = 0.5 / math.sqrt(3.0 * plane * spaces)
    result = call(
        functools.partial(insertion_kernel, scaling=scaling),
        shape((2, moms, count, block, columns), F32),
        [VMEM] + [VMEM] * len(blocks),
        10**8,
        outs=HBM,
        scratch_shapes=[
            pltpu.VMEM((moms, 16, 2, block, columns), F32),
            pltpu.VMEM((moms, 2, count, block, columns), F32),
            pltpu.SemaphoreType.DMA((moms,)),
        ],
    )(places, *blocks)
    return result.reshape(2, moms, count, 1, block, columns)


def solution(mesh):
    in_specs = (
        P("parts", "tm", None, "spin", None, "space", None),
        P("parts", "tm", None, "spin", None, "space", None),
        P("parts", None, None, None, "tm", "space", None),
        P(),
        P(),
    )
    out_specs = P("parts", None, None, "tm", "space", "spin")
    return jax.shard_map(body, mesh=mesh, in_specs=in_specs, out_specs=out_specs, check_vma=False)
```

profile of v0, /device:TPU:0, one launch (start us, length us, event | category | flops | bytes accessed | tf_op | source)
XLA Modules:
  0.0 24.9 jit_solution(5476547313172049649)
XLA Ops:
  0.0 0.5 %collective-permute-start = (bf16[24,32,128]{2,1,0:T(8,128)(2,1)}, bf16[24,32,128]{2,1,0:T(8,128)(2,1)S(1)}, u32[]{:S(2)}, u32[]{:S(2)}) collective-permute-start(bf16[24,32,128]{2,1,0:T(8,128)(2,1)} %bitcast.21), channel_id=1, source_target_pairs={{0,1},{1,0},{2,3},{3,2},{4,5},{5,4},{6,7},{7,6},{8,9},{9,8},{10,11... | collective-permute-start | bytes 589832 | tf_op jit(solution)/shard_map/ppermute | solution.py:388
  0.5 1.1 %shard_map.55 = (bf16[12,32,128]{2,1,0:T(8,128)(2,1)S(1)}, bf16[12,32,128]{2,1,0:T(8,128)(2,1)S(1)}, bf16[24,32,128]{2,1,0:T(8,128)(2,1)S(1)}, bf16[27,2,128]{2,1,0:T(2,128)(2,1)S(1)}) custom-call(bf16[24,32,128]{2,1,0:T(8,128)(2,1)} %bitcast.20, bf16[27,2,128]{2,1,0:T(2,128)(2,1)} %bitcast.23), custom_call_target="tpu_custom_call" | custom-call | flops 10000000 | bytes 1048576 | tf_op jit(solution)/shard_map/pallas_call | solution.py:426
  1.6 4.6 %collective-permute-start.1 = (bf16[12,32,128]{2,1,0:T(8,128)(2,1)S(1)}, bf16[12,32,128]{2,1,0:T(8,128)(2,1)S(1)}, u32[]{:S(2)}, u32[]{:S(2)}) collective-permute-start(bf16[12,32,128]{2,1,0:T(8,128)(2,1)S(1)} %get-tuple-element.22), channel_id=1, source_target_pairs={{0,12},{4,0},{8,4},{12,8},{1,13},{5,1},{9,5},{13,9},{2,14},{6,2},{... | collective-permute-start | bytes 294920 | tf_op jit(solution)/shard_map/ppermute | solution.py:388
  6.2 0.0 collective-permute-start.2
  6.2 0.0 collective-permute-done.other_ref
  6.2 1.4 %shard_map.56 = (f32[24,32,128]{2,1,0:T(8,128)S(1)}, bf16[768,768]{1,0:T(8,128)(2,1)S(1)}, s32[16,128]{1,0:T(8,128)S(1)}) custom-call(s32[3,3]{1,0:T(4,128)} %momenta_hbm.1, bf16[24,32,128]{2,1,0:T(8,128)(2,1)} %bitcast.22, s32[16]{0:T(128)} %list_hbm.1, bf16[24,32,128]{2,1,0:T(8,128)(2,1)S(1)} %get-tuple-element.17.fwd_ref, ...), custom_call_target="tpu_custom_call" | custom-call | flops 100000000 | bytes 1048576 | tf_op jit(solution)/shard_map/pallas_call | solution.py:436
  7.6 1.8 %collective-permute-done.1.ahead_ref = bf16[12,32,128]{2,1,0:T(8,128)(2,1)S(1)} collective-permute-done((bf16[12,32,128]{2,1,0:T(8,128)(2,1)S(1)}, bf16[12,32,128]{2,1,0:T(8,128)(2,1)S(1)}, u32[]{:S(2)}, u32[]{:S(2)}) %collective-permute-start.1) | collective-permute-done | bytes 98336 | tf_op jit(solution)/shard_map/ppermute | solution.py:388
  9.4 3.5 %collective-permute-done.2.behind_ref = bf16[12,32,128]{2,1,0:T(8,128)(2,1)S(1)} collective-permute-done((bf16[12,32,128]{2,1,0:T(8,128)(2,1)S(1)}, bf16[12,32,128]{2,1,0:T(8,128)(2,1)S(1)}, u32[]{:S(2)}, u32[]{:S(2)}) %collective-permute-start.2) | collective-permute-done | bytes 98336 | tf_op jit(solution)/shard_map/ppermute | solution.py:388
  12.9 0.5 %shard_map.57 = (bf16[256,768]{1,0:T(8,128)(2,1)S(1)}, bf16[64,768]{1,0:T(8,128)(2,1)S(1)}) custom-call(f32[24,32,128]{2,1,0:T(8,128)S(1)} %get-tuple-element.21.weave_ref, bf16[12,32,128]{2,1,0:T(8,128)(2,1)S(1)} %collective-permute-done.1.ahead_ref, bf16[12,32,128]{2,1,0:T(8,128)(2,1)S(1)} %collective-permute-done.2.behind_ref, ...), custom_call_target="tpu_custom_call" | custom-call | flops 1000000000 | bytes 1048576 | tf_op jit(solution)/shard_map/pallas_call | solution.py:456
  13.4 0.5 %shard_map.58 = (f32[64,768]{1,0:T(8,128)S(1)}, bf16[64,768]{1,0:T(8,128)(2,1)S(1)}, bf16[64,768]{1,0:T(8,128)(2,1)S(1)}) custom-call(bf16[768,768]{1,0:T(8,128)(2,1)S(1)} %get-tuple-element.20.left_ref, bf16[256,768]{1,0:T(8,128)(2,1)S(1)} %get-tuple-element.24.right_ref), custom_call_target="tpu_custom_call" | custom-call | flops 1000000000 | bytes 1048576 | tf_op jit(solution)/shard_map/pallas_call | solution.py:463
  13.9 0.1 collective-permute-start.4
  14.0 3.0 %collective-permute-start.5 = (bf16[64,768]{1,0:T(8,128)(2,1)S(1)}, bf16[64,768]{1,0:T(8,128)(2,1)S(1)}, u32[]{:S(2)}, u32[]{:S(2)}) collective-permute-start(bf16[64,768]{1,0:T(8,128)(2,1)S(1)} %get-tuple-element.28), channel_id=1, source_target_pairs={{0,12},{4,0},{8,4},{12,8},{1,13},{5,1},{9,5},{13,9},{2,14},{6,2},{... | collective-permute-start | bytes 294920 | tf_op jit(solution)/shard_map/ppermute | solution.py:388
  16.9 0.0 collective-permute-start.3
  16.9 6.7 %collective-permute-done.4 = bf16[64,768]{1,0:T(8,128)(2,1)S(1)} collective-permute-done((bf16[64,768]{1,0:T(8,128)(2,1)S(1)}, bf16[64,768]{1,0:T(8,128)(2,1)S(1)}, u32[]{:S(2)}, u32[]{:S(2)}) %collective-permute-start.4) | collective-permute-done | bytes 98336 | tf_op jit(solution)/shard_map/ppermute | solution.py:388
  23.7 0.0 collective-permute-done.5
  23.7 0.0 collective-permute-done.3
  23.7 1.2 %shard_map.59 = f32[2,3,16,16,32]{4,3,2,1,0:T(8,128)} custom-call(s32[16,128]{1,0:T(8,128)S(1)} %get-tuple-element.19.places_ref, f32[1,64,768]{2,1,0:T(8,128)S(1)} %bitcast.16, bf16[1,64,768]{2,1,0:T(8,128)(2,1)S(1)} %bitcast.19, bf16[1,64,768]{2,1,0:T(8,128)(2,1)S(1)} %bitcast.17, bf16[1,64,768]{2,1,0:T(8,128)(2,1)S(1)} %bitcast.18), custom_call_target="tpu_custom_call" | custom-call | flops 100000000 | bytes 1048576 | tf_op jit(solution)/shard_map/pallas_call | solution.py:478
Async XLA Ops:
  0.0 6.2 %collective-permute-start = (bf16[24,32,128]{2,1,0:T(8,128)(2,1)}, bf16[24,32,128]{2,1,0:T(8,128)(2,1)S(1)}, u32[]{:S(2)}, u32[]{:S(2)}) collective-permute-start(bf16[24,32,128]{2,1,0:T(8,128)(2,1)} %bitcast.21), channel_id=1, source_target_pairs={{0,1},{1,0},{2,3},{3,2},{4,5},{5,4},{6,7},{7,6},{8,9},{9,8},{10,11... | collective-permute-start | bytes 589832 | tf_op jit(solution)/shard_map/ppermute | solution.py:388
  1.6 7.9 %collective-permute-start.1 = (bf16[12,32,128]{2,1,0:T(8,128)(2,1)S(1)}, bf16[12,32,128]{2,1,0:T(8,128)(2,1)S(1)}, u32[]{:S(2)}, u32[]{:S(2)}) collective-permute-start(bf16[12,32,128]{2,1,0:T(8,128)(2,1)S(1)} %get-tuple-element.22), channel_id=1, source_target_pairs={{0,12},{4,0},{8,4},{12,8},{1,13},{5,1},{9,5},{13,9},{2,14},{6,2},{... | collective-permute-start | bytes 294920 | tf_op jit(solution)/shard_map/ppermute | solution.py:388
  6.2 6.7 %collective-permute-start.2 = (bf16[12,32,128]{2,1,0:T(8,128)(2,1)S(1)}, bf16[12,32,128]{2,1,0:T(8,128)(2,1)S(1)}, u32[]{:S(2)}, u32[]{:S(2)}) collective-permute-start(bf16[12,32,128]{2,1,0:T(8,128)(2,1)S(1)} %get-tuple-element.23), channel_id=1, source_target_pairs={{0,4},{4,8},{8,12},{12,0},{1,5},{5,9},{9,13},{13,1},{2,6},{6,10},{... | collective-permute-start | bytes 294920 | tf_op jit(solution)/shard_map/ppermute | solution.py:388
  13.9 9.8 %collective-permute-start.4 = (bf16[64,768]{1,0:T(8,128)(2,1)S(1)}, bf16[64,768]{1,0:T(8,128)(2,1)S(1)}, u32[]{:S(2)}, u32[]{:S(2)}) collective-permute-start(bf16[64,768]{1,0:T(8,128)(2,1)S(1)} %get-tuple-element.27), channel_id=1, source_target_pairs={{0,8},{4,12},{8,0},{12,4},{1,9},{5,13},{9,1},{13,5},{2,10},{6,14},... | collective-permute-start | bytes 294920 | tf_op jit(solution)/shard_map/ppermute | solution.py:388
  14.0 9.7 %collective-permute-start.5 = (bf16[64,768]{1,0:T(8,128)(2,1)S(1)}, bf16[64,768]{1,0:T(8,128)(2,1)S(1)}, u32[]{:S(2)}, u32[]{:S(2)}) collective-permute-start(bf16[64,768]{1,0:T(8,128)(2,1)S(1)} %get-tuple-element.28), channel_id=1, source_target_pairs={{0,12},{4,0},{8,4},{12,8},{1,13},{5,1},{9,5},{13,9},{2,14},{6,2},{... | collective-permute-start | bytes 294920 | tf_op jit(solution)/shard_map/ppermute | solution.py:388
  16.9 6.7 %collective-permute-start.3 = (bf16[64,768]{1,0:T(8,128)(2,1)S(1)}, bf16[64,768]{1,0:T(8,128)(2,1)S(1)}, u32[]{:S(2)}, u32[]{:S(2)}) collective-permute-start(bf16[64,768]{1,0:T(8,128)(2,1)S(1)} %get-tuple-element.26), channel_id=1, source_target_pairs={{0,4},{4,8},{8,12},{12,0},{1,5},{5,9},{9,13},{13,1},{2,6},{6,10},{... | collective-permute-start | bytes 294920 | tf_op jit(solution)/shard_map/ppermute | solution.py:388
where the time goes:
time: 25.1 us; the launch traced here: 24.9 us
  waiting for transfers between devices  12.1 us (48%)
  starting transfers between devices  8.19 us (33%)
  Pallas kernels  4.63 us (18%)
    ppermute x6, waiting for transfers between devices, passed_along(): return lax.ppermute(value, axis, pairs)  12.1 us
    ppermute x6, starting transfers between devices, passed_along(): return lax.ppermute(value, axis, pairs)  8.19 us
    pallas_call x1, Pallas kernels, body(): call(functools.partial(local_kernel, width=LX, spaces=spaces, ordered=ord...  1.39 us
    pallas_call x1, Pallas kernels, body(): call(functools.partial(insertion_kernel, scaling=scaling), shape((2, moms...  1.23 us
    pallas_call x1, Pallas kernels, body(): call(halo_kernel, [half, half] + [shape(v.shape, v.dtype) for v in (fwd,...  1.07 us
  transfers between devices with their start and end apart: 6, of which 3 were waited for; matrix products, arithmetic and copies ran while one was open for 0% of the time, Pallas kernels for 10%

commit v1 on v0

--- a/solution.py
+++ b/solution.py
@@ -161,6 +161,30 @@
     over_rows(fwd_ref.shape[1], 16, rows_body)
 
 
+SIGNS = [[1, 1, 1, 1], [1, -1, 1, -1], [1, 1, -1, -1], [1, -1, -1, 1]]
+
+
+def unit_sum(q, j):
+    x, y = {0: (0, 0), 3: (1, 0), 2: (0, 1), 1: (1, 1)}[j]
+    first, third = q & 1, q >> 1
+    matrix = BASIS[first | (first ^ x) << 1 | third << 2 | (third ^ y) << 3]
+    values = [complex(matrix[s, s ^ j]) for s in range(4)]
+    return (SIGNS.index([round((v / values[0]).real) for v in values]), values[0])
+
+
+def times_unit(unit, value):
+    real, imag = value
+    if unit == 1:
+        return (real, imag)
+    if unit == -1:
+        return (-real, -imag)
+    return (-imag, real) if unit == 1j else (imag, -real)
+
+
+def ring_place(place):
+    return place ^ (place >> 1)
+
+
 def table_place(number):
     x = (number ^ (number >> 1)) & 1
     y = ((number >> 2) ^ (number >> 3)) & 1
@@ -239,7 +263,9 @@
         for number in range(columns // block):
             spinor = spinor_reader(source_ref, pl.ds(number * block, block))
             if ordered:
-                k = (half * (columns // block) + number - z_place + spaces) % spaces
+                target = half * (columns // block) + number
+                k = (ring_place(target) - ring_place(z_place) + spaces) % spaces
+                k = jnp.where(k > 1, spaces + 1 - k, k)
                 rotate(spinor, k * moms * 4 * block, 4 * block, block)
             else:
                 rotate(spinor, half * columns, 8 * columns, 2 * columns)
@@ -266,34 +292,47 @@
 ):
     columns, plane = weave_ref.shape[1:]
     wide = 4 * columns
+    gamma_columns, units = unit_rows(SINGLES[2])
+    step = 16
+
+    def one_colour(c, links, first_row):
+        rows = pl.ds(first_row, step)
+
+        def half(ref, s, d):
+            return tuple(ref[half_part(ri, s, d), rows].astype(F32) for ri in range(2))
+
+        hops = []
+        for s in range(2):
+            real = imag = None
+            for d in range(3):
+                u_real, u_imag = links[d]
+                h_real, h_imag = half(ahead_ref, s, d)
+                part_real = u_real * h_real - u_imag * h_imag
+                part_imag = u_real * h_imag + u_imag * h_real
+                real = part_real if real is None else real + part_real
+                imag = part_imag if imag is None else imag + part_imag
+            back = half(behind_ref, s, c)
+            hops.append((plus_unit((real, imag), -1, back), plus_unit((real, imag), 1, back)))
+        for s in range(4):
+            total = (weave_ref[part(0, s, c), rows], weave_ref[part(1, s, c), rows])
+            if s < 2:
+                real, imag = plus_unit(total, 1, hops[s][0])
+            else:
+                real, imag = plus_unit(total, -units[s], hops[gamma_columns[s]][1])
+            at_real = pl.ds(s * columns + first_row, step)
+            at_imag = pl.ds(wide + s * columns + first_row, step)
+            first = pl.ds(c * plane, plane)
+            second = pl.ds((3 + c) * plane, plane)
+            right_ref[at_real, first] = real.astype(BF16)
+            right_ref[at_real, second] = imag.astype(BF16)
+            right_ref[at_imag, first] = imag.astype(BF16)
+            right_ref[at_imag, second] = (-real).astype(BF16)
+
     link = link_reader(links_ref, 2)
-
-    def half_reader(ref, rows):
-        return [
-            [tuple(ref[half_part(ri, s, c), rows].astype(F32) for ri in range(2)) for c in range(3)]
-            for s in range(2)
-        ]
-
-    def rows_body(rows):
-        total = [
-            [(weave_ref[part(0, s, c), rows], weave_ref[part(1, s, c), rows]) for c in range(3)]
-            for s in range(4)
-        ]
-        add_hop(total, colour_product(link, half_reader(ahead_ref, rows), False), 2, -1, 1)
-        add_hop(total, half_reader(behind_ref, rows), 2, 1, -1)
-        for s in range(4):
-            at_real = pl.ds(pl.multiple_of(s * columns + rows.start, 8), rows.size)
-            at_imag = pl.ds(pl.multiple_of(wide + s * columns + rows.start, 8), rows.size)
-            for c in range(3):
-                real, imag = total[s][c]
-                first = pl.ds(c * plane, plane)
-                second = pl.ds((3 + c) * plane, plane)
-                right_ref[at_real, first] = real.astype(BF16)
-                right_ref[at_real, second] = imag.astype(BF16)
-                right_ref[at_imag, first] = imag.astype(BF16)
-                right_ref[at_imag, second] = (-real).astype(BF16)
-
-    over_rows(columns, 8, rows_body)
+    for c in range(3):
+        links = [link(c, d) for d in range(3)]
+        for first_row in range(0, columns, step):
+            one_colour(c, links, first_row)
     multiply(left_ref, right_ref, [out_ref], first_block, moms)
 
 
@@ -308,25 +347,6 @@
     moms, _, count, block, columns = out_ref.shape
     wide = 4 * columns
     group = lax.broadcasted_iota(jnp.int32, (1, wide), 1) // columns
-
-    def by_group(values):
-        result = jnp.full((1, wide), values[0], F32)
-        for j in range(1, 4):
-            result = jnp.where(group == j, values[j], result)
-        return result
-
-    weights = []
-    for q in range(4):
-        rows = []
-        for s in range(4):
-            units = []
-            for j in range(4):
-                x, y = {0: (0, 0), 3: (1, 0), 2: (0, 1), 1: (1, 1)}[j]
-                first, third = q & 1, q >> 1
-                number = first | (first ^ x) << 1 | third << 2 | (third ^ y) << 3
-                units.append(complex(BASIS[number][s, s ^ j]) * scaling)
-            rows.append((by_group([u.real for u in units]), by_group([u.imag for u in units])))
-        weights.append(rows)
 
     even = group % 2 == 0
 
@@ -354,20 +374,18 @@
                         total = term if total is None else total + term
                 both.append(crossed(total, s))
             spins.append(both)
-        for q in range(4):
-            real = imag = None
-            for s in range(4):
-                w_real, w_imag = weights[q][s]
-                a, b = spins[s]
-                part_real = w_real * a - w_imag * b
-                part_imag = w_real * b + w_imag * a
-                real = part_real if real is None else real + part_real
-                imag = part_imag if imag is None else imag + part_imag
-            for j in range(4):
-                for ri, value in enumerate((real, imag)):
-                    if j:
-                        value = pltpu.roll(value, wide - j * columns, 1)
-                    table_ref[p, 4 * q + j, ri] = value[:, :columns]
+        sums = [[], []]
+        for ri in range(2):
+            a, b, c, d = (spins[s][ri] * scaling for s in range(4))
+            near, far = (a + b, a - b), (c + d, c - d)
+            sums[ri] = [near[0] + far[0], near[1] + far[1], near[0] - far[0], near[1] - far[1]]
+        for j in range(4):
+            moved = [[v if j == 0 else pltpu.roll(v, wide - j * columns, 1) for v in r] for r in sums]
+            for q in range(4):
+                number, unit = unit_sum(q, j)
+                value = times_unit(unit, (moved[0][number], moved[1][number]))
+                for ri in range(2):
+                    table_ref[p, 4 * q + j, ri] = value[ri][:, :columns]
         for k in range(count):
             for ri in range(2):
                 out_ref[p, ri, k] = table_ref[p, places[k], ri]
@@ -385,6 +403,14 @@
 def passed_along(value, axis, steps):
     count = lax.axis_size(axis)
     pairs = [(source, (source + steps) % count) for source in range(count)]
+    return lax.ppermute(value, axis, pairs)
+
+
+def passed_around(value, axis, number):
+    count = lax.axis_size(axis)
+    steps = 1 if number == 1 else count + 1 - number
+    at = {ring_place(device): device for device in range(count)}
+    pairs = [(at[place], at[(place + steps) % count]) for place in range(count)]
     return lax.ppermute(value, axis, pairs)
 
 
@@ -468,7 +494,7 @@
         )(left, right)
         blocks = [own_pairs]
         for k, value in enumerate([first, *others], 1):
-            blocks.append(passed_along(value, "space", k))
+            blocks.append(passed_around(value, "space", k))
         blocks = [b[None] for b in blocks]
     else:
         split = first.reshape(4, spaces, block, moms * wide)

time: 25.1 us -> 26.8 us (1.068)
  waiting for transfers between devices: 12.1 us -> 13.9 us
    ppermute x0 -> x3, waiting for transfers between devices: none -> 8.57 us  [passed_around(): return lax.ppermute(value, axis, pairs)]
    ppermute x6 -> x3, waiting for transfers between devices: 12.1 us -> 5.32 us  [passed_along(): return lax.ppermute(value, axis, pairs)]
    ppermute x6 -> x3, starting transfers between devices: 8.19 us -> 5.14 us  [passed_along(): return lax.ppermute(value, axis, pairs)]
    ppermute x0 -> x3, starting transfers between devices: none -> 3.04 us  [passed_around(): return lax.ppermute(value, axis, pairs)]
  transfers between devices with their start and end apart: 6 -> 6, of which waited for: 3 -> 5; matrix products, arithmetic and copies ran while one was open for 0% -> 0% of each run, Pallas kernels for 10% -> 9%
where the time goes in v1:
time: 26.8 us; the launch traced here: 26.7 us
  waiting for transfers between devices  13.9 us (52%)
  starting transfers between devices  8.18 us (31%)
  Pallas kernels  4.56 us (17%)
    ppermute x3, waiting for transfers between devices, passed_around(): return lax.ppermute(value, axis, pairs)  8.57 us
    ppermute x3, waiting for transfers between devices, passed_along(): return lax.ppermute(value, axis, pairs)  5.32 us
    ppermute x3, starting transfers between devices, passed_along(): return lax.ppermute(value, axis, pairs)  5.14 us
    ppermute x3, starting transfers between devices, passed_around(): return lax.ppermute(value, axis, pairs)  3.04 us
    pallas_call x1, Pallas kernels, body(): call(functools.partial(local_kernel, width=LX, spaces=spaces, ordered=ord...  1.4 us
    pallas_call x1, Pallas kernels, body(): call(functools.partial(insertion_kernel, scaling=scaling), shape((2, moms...  1.22 us
    pallas_call x1, Pallas kernels, body(): call(halo_kernel, [half, half] + [shape(v.shape, v.dtype) for v in (fwd,...  1.07 us
  transfers between devices with their start and end apart: 6, of which 5 were waited for; matrix products, arithmetic and copies ran while one was open for 0% of the time, Pallas kernels for 9%

profile of v1, /device:TPU:0, one launch (start us, length us, event | category | flops | bytes accessed | tf_op | source)
XLA Modules:
  0.0 26.7 jit_solution(18140325969750911939)
XLA Ops:
  0.0 0.5 %collective-permute-start = (bf16[24,32,128]{2,1,0:T(8,128)(2,1)}, bf16[24,32,128]{2,1,0:T(8,128)(2,1)S(1)}, u32[]{:S(2)}, u32[]{:S(2)}) collective-permute-start(bf16[24,32,128]{2,1,0:T(8,128)(2,1)} %bitcast.21), channel_id=1, source_target_pairs={{0,1},{1,0},{2,3},{3,2},{4,5},{5,4},{6,7},{7,6},{8,9},{9,8},{10,11... | collective-permute-start | bytes 589832 | tf_op jit(solution)/shard_map/ppermute | solution.py:406
  0.5 1.1 %shard_map.55 = (bf16[12,32,128]{2,1,0:T(8,128)(2,1)S(1)}, bf16[12,32,128]{2,1,0:T(8,128)(2,1)S(1)}, bf16[24,32,128]{2,1,0:T(8,128)(2,1)S(1)}, bf16[27,2,128]{2,1,0:T(2,128)(2,1)S(1)}) custom-call(bf16[24,32,128]{2,1,0:T(8,128)(2,1)} %bitcast.20, bf16[27,2,128]{2,1,0:T(2,128)(2,1)} %bitcast.23), custom_call_target="tpu_custom_call" | custom-call | flops 10000000 | bytes 1048576 | tf_op jit(solution)/shard_map/pallas_call | solution.py:452
  1.6 4.6 %collective-permute-start.1 = (bf16[12,32,128]{2,1,0:T(8,128)(2,1)S(1)}, bf16[12,32,128]{2,1,0:T(8,128)(2,1)S(1)}, u32[]{:S(2)}, u32[]{:S(2)}) collective-permute-start(bf16[12,32,128]{2,1,0:T(8,128)(2,1)S(1)} %get-tuple-element.22), channel_id=1, source_target_pairs={{0,12},{4,0},{8,4},{12,8},{1,13},{5,1},{9,5},{13,9},{2,14},{6,2},{... | collective-permute-start | bytes 294920 | tf_op jit(solution)/shard_map/ppermute | solution.py:406
  6.2 0.0 collective-permute-start.2
  6.2 0.0 collective-permute-done.other_ref
  6.2 1.4 %shard_map.56 = (f32[24,32,128]{2,1,0:T(8,128)S(1)}, bf16[768,768]{1,0:T(8,128)(2,1)S(1)}, s32[16,128]{1,0:T(8,128)S(1)}) custom-call(s32[3,3]{1,0:T(4,128)} %momenta_hbm.1, bf16[24,32,128]{2,1,0:T(8,128)(2,1)} %bitcast.22, s32[16]{0:T(128)} %list_hbm.1, bf16[24,32,128]{2,1,0:T(8,128)(2,1)S(1)} %get-tuple-element.17.fwd_ref, ...), custom_call_target="tpu_custom_call" | custom-call | flops 100000000 | bytes 1048576 | tf_op jit(solution)/shard_map/pallas_call | solution.py:462
  7.6 1.8 %collective-permute-done.1.ahead_ref = bf16[12,32,128]{2,1,0:T(8,128)(2,1)S(1)} collective-permute-done((bf16[12,32,128]{2,1,0:T(8,128)(2,1)S(1)}, bf16[12,32,128]{2,1,0:T(8,128)(2,1)S(1)}, u32[]{:S(2)}, u32[]{:S(2)}) %collective-permute-start.1) | collective-permute-done | bytes 98336 | tf_op jit(solution)/shard_map/ppermute | solution.py:406
  9.4 3.5 %collective-permute-done.2.behind_ref = bf16[12,32,128]{2,1,0:T(8,128)(2,1)S(1)} collective-permute-done((bf16[12,32,128]{2,1,0:T(8,128)(2,1)S(1)}, bf16[12,32,128]{2,1,0:T(8,128)(2,1)S(1)}, u32[]{:S(2)}, u32[]{:S(2)}) %collective-permute-start.2) | collective-permute-done | bytes 98336 | tf_op jit(solution)/shard_map/ppermute | solution.py:406
  12.9 0.4 %shard_map.57 = (bf16[256,768]{1,0:T(8,128)(2,1)S(1)}, bf16[64,768]{1,0:T(8,128)(2,1)S(1)}) custom-call(f32[24,32,128]{2,1,0:T(8,128)S(1)} %get-tuple-element.21.weave_ref, bf16[12,32,128]{2,1,0:T(8,128)(2,1)S(1)} %collective-permute-done.1.ahead_ref, bf16[12,32,128]{2,1,0:T(8,128)(2,1)S(1)} %collective-permute-done.2.behind_ref, ...), custom_call_target="tpu_custom_call" | custom-call | flops 1000000000 | bytes 1048576 | tf_op jit(solution)/shard_map/pallas_call | solution.py:482
  13.4 0.5 %shard_map.58 = (f32[64,768]{1,0:T(8,128)S(1)}, bf16[64,768]{1,0:T(8,128)(2,1)S(1)}, bf16[64,768]{1,0:T(8,128)(2,1)S(1)}) custom-call(bf16[768,768]{1,0:T(8,128)(2,1)S(1)} %get-tuple-element.20.left_ref, bf16[256,768]{1,0:T(8,128)(2,1)S(1)} %get-tuple-element.24.right_ref), custom_call_target="tpu_custom_call" | custom-call | flops 1000000000 | bytes 1048576 | tf_op jit(solution)/shard_map/pallas_call | solution.py:489
  13.8 0.1 collective-permute-start.4
  13.9 3.0 %collective-permute-start.5 = (bf16[64,768]{1,0:T(8,128)(2,1)S(1)}, bf16[64,768]{1,0:T(8,128)(2,1)S(1)}, u32[]{:S(2)}, u32[]{:S(2)}) collective-permute-start(bf16[64,768]{1,0:T(8,128)(2,1)S(1)} %get-tuple-element.28), channel_id=1, source_target_pairs={{0,12},{4,8},{12,0},{8,4},{1,13},{5,9},{13,1},{9,5},{2,14},{6,10},... | collective-permute-start | bytes 294920 | tf_op jit(solution)/shard_map/ppermute | solution.py:414
  16.9 0.0 collective-permute-start.3
  16.9 2.1 %collective-permute-done.4 = bf16[64,768]{1,0:T(8,128)(2,1)S(1)} collective-permute-done((bf16[64,768]{1,0:T(8,128)(2,1)S(1)}, bf16[64,768]{1,0:T(8,128)(2,1)S(1)}, u32[]{:S(2)}, u32[]{:S(2)}) %collective-permute-start.4) | collective-permute-done | bytes 98336 | tf_op jit(solution)/shard_map/ppermute | solution.py:414
  19.0 3.5 %collective-permute-done.5 = bf16[64,768]{1,0:T(8,128)(2,1)S(1)} collective-permute-done((bf16[64,768]{1,0:T(8,128)(2,1)S(1)}, bf16[64,768]{1,0:T(8,128)(2,1)S(1)}, u32[]{:S(2)}, u32[]{:S(2)}) %collective-permute-start.5) | collective-permute-done | bytes 98336 | tf_op jit(solution)/shard_map/ppermute | solution.py:414
  22.4 3.0 %collective-permute-done.3 = bf16[64,768]{1,0:T(8,128)(2,1)S(1)} collective-permute-done((bf16[64,768]{1,0:T(8,128)(2,1)S(1)}, bf16[64,768]{1,0:T(8,128)(2,1)S(1)}, u32[]{:S(2)}, u32[]{:S(2)}) %collective-permute-start.3) | collective-permute-done | bytes 98336 | tf_op jit(solution)/shard_map/ppermute | solution.py:414
  25.4 1.2 %shard_map.59 = f32[2,3,16,16,32]{4,3,2,1,0:T(8,128)} custom-call(s32[16,128]{1,0:T(8,128)S(1)} %get-tuple-element.19.places_ref, f32[1,64,768]{2,1,0:T(8,128)S(1)} %bitcast.16, bf16[1,64,768]{2,1,0:T(8,128)(2,1)S(1)} %bitcast.19, bf16[1,64,768]{2,1,0:T(8,128)(2,1)S(1)} %bitcast.17, bf16[1,64,768]{2,1,0:T(8,128)(2,1)S(1)} %bitcast.18), custom_call_target="tpu_custom_call" | custom-call | flops 100000000 | bytes 1048576 | tf_op jit(solution)/shard_map/pallas_call | solution.py:504
Async XLA Ops:
  0.0 6.2 %collective-permute-start = (bf16[24,32,128]{2,1,0:T(8,128)(2,1)}, bf16[24,32,128]{2,1,0:T(8,128)(2,1)S(1)}, u32[]{:S(2)}, u32[]{:S(2)}) collective-permute-start(bf16[24,32,128]{2,1,0:T(8,128)(2,1)} %bitcast.21), channel_id=1, source_target_pairs={{0,1},{1,0},{2,3},{3,2},{4,5},{5,4},{6,7},{7,6},{8,9},{9,8},{10,11... | collective-permute-start | bytes 589832 | tf_op jit(solution)/shard_map/ppermute | solution.py:406
  1.6 7.9 %collective-permute-start.1 = (bf16[12,32,128]{2,1,0:T(8,128)(2,1)S(1)}, bf16[12,32,128]{2,1,0:T(8,128)(2,1)S(1)}, u32[]{:S(2)}, u32[]{:S(2)}) collective-permute-start(bf16[12,32,128]{2,1,0:T(8,128)(2,1)S(1)} %get-tuple-element.22), channel_id=1, source_target_pairs={{0,12},{4,0},{8,4},{12,8},{1,13},{5,1},{9,5},{13,9},{2,14},{6,2},{... | collective-permute-start | bytes 294920 | tf_op jit(solution)/shard_map/ppermute | solution.py:406
  6.2 6.7 %collective-permute-start.2 = (bf16[12,32,128]{2,1,0:T(8,128)(2,1)S(1)}, bf16[12,32,128]{2,1,0:T(8,128)(2,1)S(1)}, u32[]{:S(2)}, u32[]{:S(2)}) collective-permute-start(bf16[12,32,128]{2,1,0:T(8,128)(2,1)S(1)} %get-tuple-element.23), channel_id=1, source_target_pairs={{0,4},{4,8},{8,12},{12,0},{1,5},{5,9},{9,13},{13,1},{2,6},{6,10},{... | collective-permute-start | bytes 294920 | tf_op jit(solution)/shard_map/ppermute | solution.py:406
  13.8 5.1 %collective-permute-start.4 = (bf16[64,768]{1,0:T(8,128)(2,1)S(1)}, bf16[64,768]{1,0:T(8,128)(2,1)S(1)}, u32[]{:S(2)}, u32[]{:S(2)}) collective-permute-start(bf16[64,768]{1,0:T(8,128)(2,1)S(1)} %get-tuple-element.27), channel_id=1, source_target_pairs={{0,8},{4,0},{12,4},{8,12},{1,9},{5,1},{13,5},{9,13},{2,10},{6,2},{... | collective-permute-start | bytes 294920 | tf_op jit(solution)/shard_map/ppermute | solution.py:414
  13.9 8.5 %collective-permute-start.5 = (bf16[64,768]{1,0:T(8,128)(2,1)S(1)}, bf16[64,768]{1,0:T(8,128)(2,1)S(1)}, u32[]{:S(2)}, u32[]{:S(2)}) collective-permute-start(bf16[64,768]{1,0:T(8,128)(2,1)S(1)} %get-tuple-element.28), channel_id=1, source_target_pairs={{0,12},{4,8},{12,0},{8,4},{1,13},{5,9},{13,1},{9,5},{2,14},{6,10},... | collective-permute-start | bytes 294920 | tf_op jit(solution)/shard_map/ppermute | solution.py:414
  16.9 8.6 %collective-permute-start.3 = (bf16[64,768]{1,0:T(8,128)(2,1)S(1)}, bf16[64,768]{1,0:T(8,128)(2,1)S(1)}, u32[]{:S(2)}, u32[]{:S(2)}) collective-permute-start(bf16[64,768]{1,0:T(8,128)(2,1)S(1)} %get-tuple-element.26), channel_id=1, source_target_pairs={{0,4},{4,12},{12,8},{8,0},{1,5},{5,13},{13,9},{9,1},{2,6},{6,14},{... | collective-permute-start | bytes 294920 | tf_op jit(solution)/shard_map/ppermute | solution.py:414

commit v2 on v1

--- a/solution.py
+++ b/solution.py
@@ -143,7 +143,10 @@
 
 
 def halo_kernel(fwd_hbm, links_hbm, up_ref, down_ref, fwd_ref, links_ref, sems):
-    for copy in copy_all(((fwd_hbm, fwd_ref), (links_hbm, links_ref)), sems):
+    count = fwd_ref.shape[0] // 4
+    quarters = [pl.ds(i * count, count) for i in range(4)]
+    pairs = [(fwd_hbm.at[quarter], fwd_ref.at[quarter]) for quarter in quarters]
+    for copy in copy_all([*pairs, (links_hbm, links_ref)], sems):
         copy.wait()
     link = link_reader(links_ref, 2)
 
@@ -336,10 +339,8 @@
     multiply(left_ref, right_ref, [out_ref], first_block, moms)
 
 
-def other_pairs_kernel(left_ref, right_ref, own_ref, *out_refs, moms):
-    multiply(left_ref, right_ref, [own_ref], 0, moms)
-    if out_refs:
-        multiply(left_ref, right_ref, out_refs, 2, moms)
+def other_pairs_kernel(left_ref, right_ref, *out_refs, first_block, moms):
+    multiply(left_ref, right_ref, out_refs, first_block, moms)
 
 
 def insertion_kernel(places_ref, *rest, scaling):
@@ -454,7 +455,7 @@
         [half, half] + [shape(v.shape, v.dtype) for v in (fwd, links)],
         [HBM] * 2,
         10**7,
-        scratch_shapes=[pltpu.SemaphoreType.DMA((2,))],
+        scratch_shapes=[pltpu.SemaphoreType.DMA((5,))],
     )(*[in_hbm(v) for v in (fwd, links)])
     behind = passed_along(to_down, "space", 1)
     ahead = passed_along(to_up, "space", -1)
@@ -486,13 +487,15 @@
         10**9,
     )(weave, ahead, behind, links_here, left)
     if ordered:
-        own_pairs, *others = call(
-            functools.partial(other_pairs_kernel, moms=moms),
-            [shape(pair_shape.shape, F32)] + [pair_shape] * (spaces - 2),
-            [VMEM] * 2,
-            10**9,
-        )(left, right)
-        blocks = [own_pairs]
+
+        def more(first_block, shapes):
+            kernel = functools.partial(other_pairs_kernel, first_block=first_block, moms=moms)
+            return call(kernel, shapes, [VMEM] * 2, 10**9)(left, right)
+
+        others = []
+        if spaces > 2:
+            others = more(2, [pair_shape] * (spaces - 2))
+        blocks = [*more(0, [shape(pair_shape.shape, F32)])]
         for k, value in enumerate([first, *others], 1):
             blocks.append(passed_around(value, "space", k))
         blocks = [b[None] for b in blocks]

time: 26.8 us -> 24.9 us (0.929)
  waiting for transfers between devices: 13.9 us -> 11 us
  starting transfers between devices: 8.18 us -> 8.96 us
    ppermute x3, waiting for transfers between devices: 8.57 us -> 5.65 us  [passed_around(): return lax.ppermute(value, axis, pairs)]
    ppermute x3, starting transfers between devices: 3.04 us -> 3.82 us  [passed_around(): return lax.ppermute(value, axis, pairs)]
    pallas_call x1 -> x2, Pallas kernels: 0.46 us -> 0.64 us  [more(): return call(kernel, shapes, [VMEM] * 2, 10 ** 9)(left, right)]
  transfers between devices with their start and end apart: 6 -> 6, of which waited for: 5 -> 3; matrix products, arithmetic and copies ran while one was open for 0% -> 0% of each run, Pallas kernels for 9% -> 12%
where the time goes in v2:
time: 24.9 us; the launch traced here: 24.7 us
  waiting for transfers between devices  11 us (44%)
  starting transfers between devices  8.96 us (36%)
  Pallas kernels  4.71 us (19%)
    ppermute x3, waiting for transfers between devices, passed_around(): return lax.ppermute(value, axis, pairs)  5.65 us
    ppermute x3, waiting for transfers between devices, passed_along(): return lax.ppermute(value, axis, pairs)  5.32 us
    ppermute x3, starting transfers between devices, passed_along(): return lax.ppermute(value, axis, pairs)  5.14 us
    ppermute x3, starting transfers between devices, passed_around(): return lax.ppermute(value, axis, pairs)  3.82 us
    pallas_call x1, Pallas kernels, body(): call(functools.partial(local_kernel, width=LX, spaces=spaces, ordered=ord...  1.4 us
    pallas_call x1, Pallas kernels, body(): call(functools.partial(insertion_kernel, scaling=scaling), shape((2, moms...  1.21 us
    pallas_call x1, Pallas kernels, body(): call(halo_kernel, [half, half] + [shape(v.shape, v.dtype) for v in (fwd,...  1.04 us
    pallas_call x2, Pallas kernels, more(): return call(kernel, shapes, [VMEM] * 2, 10 ** 9)(left, right)  0.64 us
  transfers between devices with their start and end apart: 6, of which 3 were waited for; matrix products, arithmetic and copies ran while one was open for 0% of the time, Pallas kernels for 12%

profile of v2, /device:TPU:0, one launch (start us, length us, event | category | flops | bytes accessed | tf_op | source)
XLA Modules:
  0.0 24.7 jit_solution(3680839451780639250)
XLA Ops:
  0.0 0.5 %collective-permute-start = (bf16[24,32,128]{2,1,0:T(8,128)(2,1)}, bf16[24,32,128]{2,1,0:T(8,128)(2,1)S(1)}, u32[]{:S(2)}, u32[]{:S(2)}) collective-permute-start(bf16[24,32,128]{2,1,0:T(8,128)(2,1)} %bitcast.21), channel_id=1, source_target_pairs={{0,1},{1,0},{2,3},{3,2},{4,5},{5,4},{6,7},{7,6},{8,9},{9,8},{10,11... | collective-permute-start | bytes 589832 | tf_op jit(solution)/shard_map/ppermute | solution.py:407
  0.5 1.0 %shard_map.55 = (bf16[12,32,128]{2,1,0:T(8,128)(2,1)S(1)}, bf16[12,32,128]{2,1,0:T(8,128)(2,1)S(1)}, bf16[24,32,128]{2,1,0:T(8,128)(2,1)S(1)}, bf16[27,2,128]{2,1,0:T(2,128)(2,1)S(1)}) custom-call(bf16[24,32,128]{2,1,0:T(8,128)(2,1)} %bitcast.20, bf16[27,2,128]{2,1,0:T(2,128)(2,1)} %bitcast.23), custom_call_target="tpu_custom_call" | custom-call | flops 10000000 | bytes 1048576 | tf_op jit(solution)/shard_map/pallas_call | solution.py:453
  1.5 4.6 %collective-permute-start.1 = (bf16[12,32,128]{2,1,0:T(8,128)(2,1)S(1)}, bf16[12,32,128]{2,1,0:T(8,128)(2,1)S(1)}, u32[]{:S(2)}, u32[]{:S(2)}) collective-permute-start(bf16[12,32,128]{2,1,0:T(8,128)(2,1)S(1)} %get-tuple-element.21), channel_id=1, source_target_pairs={{0,12},{4,0},{8,4},{12,8},{1,13},{5,1},{9,5},{13,9},{2,14},{6,2},{... | collective-permute-start | bytes 294920 | tf_op jit(solution)/shard_map/ppermute | solution.py:407
  6.2 0.0 collective-permute-start.2
  6.2 0.0 collective-permute-done.other_ref
  6.2 1.4 %shard_map.56 = (f32[24,32,128]{2,1,0:T(8,128)S(1)}, bf16[768,768]{1,0:T(8,128)(2,1)S(1)}, s32[16,128]{1,0:T(8,128)S(1)}) custom-call(s32[3,3]{1,0:T(4,128)} %momenta_hbm.1, bf16[24,32,128]{2,1,0:T(8,128)(2,1)} %bitcast.22, s32[16]{0:T(128)} %list_hbm.1, bf16[24,32,128]{2,1,0:T(8,128)(2,1)S(1)} %get-tuple-element.16.fwd_ref, ...), custom_call_target="tpu_custom_call" | custom-call | flops 100000000 | bytes 1048576 | tf_op jit(solution)/shard_map/pallas_call | solution.py:463
  7.6 1.8 %collective-permute-done.1.ahead_ref = bf16[12,32,128]{2,1,0:T(8,128)(2,1)S(1)} collective-permute-done((bf16[12,32,128]{2,1,0:T(8,128)(2,1)S(1)}, bf16[12,32,128]{2,1,0:T(8,128)(2,1)S(1)}, u32[]{:S(2)}, u32[]{:S(2)}) %collective-permute-start.1) | collective-permute-done | bytes 98336 | tf_op jit(solution)/shard_map/ppermute | solution.py:407
  9.4 3.5 %collective-permute-done.2.behind_ref = bf16[12,32,128]{2,1,0:T(8,128)(2,1)S(1)} collective-permute-done((bf16[12,32,128]{2,1,0:T(8,128)(2,1)S(1)}, bf16[12,32,128]{2,1,0:T(8,128)(2,1)S(1)}, u32[]{:S(2)}, u32[]{:S(2)}) %collective-permute-start.2) | collective-permute-done | bytes 98336 | tf_op jit(solution)/shard_map/ppermute | solution.py:407
  12.9 0.4 %shard_map.57 = (bf16[256,768]{1,0:T(8,128)(2,1)S(1)}, bf16[64,768]{1,0:T(8,128)(2,1)S(1)}) custom-call(f32[24,32,128]{2,1,0:T(8,128)S(1)} %get-tuple-element.20.weave_ref, bf16[12,32,128]{2,1,0:T(8,128)(2,1)S(1)} %collective-permute-done.1.ahead_ref, bf16[12,32,128]{2,1,0:T(8,128)(2,1)S(1)} %collective-permute-done.2.behind_ref, ...), custom_call_target="tpu_custom_call" | custom-call | flops 1000000000 | bytes 1048576 | tf_op jit(solution)/shard_map/pallas_call | solution.py:483
  13.3 0.7 %collective-permute-start.3 = (bf16[64,768]{1,0:T(8,128)(2,1)S(1)}, bf16[64,768]{1,0:T(8,128)(2,1)S(1)}, u32[]{:S(2)}, u32[]{:S(2)}) collective-permute-start(bf16[64,768]{1,0:T(8,128)(2,1)S(1)} %get-tuple-element.24), channel_id=1, source_target_pairs={{0,4},{4,12},{12,8},{8,0},{1,5},{5,13},{13,9},{9,1},{2,6},{6,14},{... | collective-permute-start | bytes 294920 | tf_op jit(solution)/shard_map/ppermute | solution.py:415
  14.0 0.3 %shard_map.59 = (bf16[64,768]{1,0:T(8,128)(2,1)S(1)}, bf16[64,768]{1,0:T(8,128)(2,1)S(1)}) custom-call(bf16[768,768]{1,0:T(8,128)(2,1)S(1)} %get-tuple-element.19.left_ref, bf16[256,768]{1,0:T(8,128)(2,1)S(1)} %get-tuple-element.23.right_ref), custom_call_target="tpu_custom_call" | custom-call | flops 1000000000 | bytes 1048576 | tf_op jit(solution)/shard_map/pallas_call | solution.py:493
  14.4 2.3 %collective-permute-start.4 = (bf16[64,768]{1,0:T(8,128)(2,1)S(1)}, bf16[64,768]{1,0:T(8,128)(2,1)S(1)}, u32[]{:S(2)}, u32[]{:S(2)}) collective-permute-start(bf16[64,768]{1,0:T(8,128)(2,1)S(1)} %get-tuple-element.25), channel_id=1, source_target_pairs={{0,8},{4,0},{12,4},{8,12},{1,9},{5,1},{13,5},{9,13},{2,10},{6,2},{... | collective-permute-start | bytes 294920 | tf_op jit(solution)/shard_map/ppermute | solution.py:415
  16.7 0.8 %collective-permute-start.5 = (bf16[64,768]{1,0:T(8,128)(2,1)S(1)}, bf16[64,768]{1,0:T(8,128)(2,1)S(1)}, u32[]{:S(2)}, u32[]{:S(2)}) collective-permute-start(bf16[64,768]{1,0:T(8,128)(2,1)S(1)} %get-tuple-element.26), channel_id=1, source_target_pairs={{0,12},{4,8},{12,0},{8,4},{1,13},{5,9},{13,1},{9,5},{2,14},{6,10},... | collective-permute-start | bytes 294920 | tf_op jit(solution)/shard_map/ppermute | solution.py:415
  17.5 0.3 %shard_map.58 = f32[64,768]{1,0:T(8,128)S(1)} custom-call(bf16[768,768]{1,0:T(8,128)(2,1)S(1)} %get-tuple-element.19.left_ref, bf16[256,768]{1,0:T(8,128)(2,1)S(1)} %get-tuple-element.23.right_ref), custom_call_target="tpu_custom_call" | custom-call | flops 1000000000 | bytes 1048576 | tf_op jit(solution)/shard_map/pallas_call | solution.py:493
  17.8 5.6 %collective-permute-done.3 = bf16[64,768]{1,0:T(8,128)(2,1)S(1)} collective-permute-done((bf16[64,768]{1,0:T(8,128)(2,1)S(1)}, bf16[64,768]{1,0:T(8,128)(2,1)S(1)}, u32[]{:S(2)}, u32[]{:S(2)}) %collective-permute-start.3) | collective-permute-done | bytes 98336 | tf_op jit(solution)/shard_map/ppermute | solution.py:415
  23.4 0.0 collective-permute-done.4
  23.5 0.0 collective-permute-done.5
  23.5 1.2 %shard_map.60 = f32[2,3,16,16,32]{4,3,2,1,0:T(8,128)} custom-call(s32[16,128]{1,0:T(8,128)S(1)} %get-tuple-element.18.places_ref, f32[1,64,768]{2,1,0:T(8,128)S(1)} %bitcast.16, bf16[1,64,768]{2,1,0:T(8,128)(2,1)S(1)} %bitcast.17, bf16[1,64,768]{2,1,0:T(8,128)(2,1)S(1)} %bitcast.18, bf16[1,64,768]{2,1,0:T(8,128)(2,1)S(1)} %bitcast.19), custom_call_target="tpu_custom_call" | custom-call | flops 100000000 | bytes 1048576 | tf_op jit(solution)/shard_map/pallas_call | solution.py:507
Async XLA Ops:
  0.0 6.2 %collective-permute-start = (bf16[24,32,128]{2,1,0:T(8,128)(2,1)}, bf16[24,32,128]{2,1,0:T(8,128)(2,1)S(1)}, u32[]{:S(2)}, u32[]{:S(2)}) collective-permute-start(bf16[24,32,128]{2,1,0:T(8,128)(2,1)} %bitcast.21), channel_id=1, source_target_pairs={{0,1},{1,0},{2,3},{3,2},{4,5},{5,4},{6,7},{7,6},{8,9},{9,8},{10,11... | collective-permute-start | bytes 589832 | tf_op jit(solution)/shard_map/ppermute | solution.py:407
  1.5 7.9 %collective-permute-start.1 = (bf16[12,32,128]{2,1,0:T(8,128)(2,1)S(1)}, bf16[12,32,128]{2,1,0:T(8,128)(2,1)S(1)}, u32[]{:S(2)}, u32[]{:S(2)}) collective-permute-start(bf16[12,32,128]{2,1,0:T(8,128)(2,1)S(1)} %get-tuple-element.21), channel_id=1, source_target_pairs={{0,12},{4,0},{8,4},{12,8},{1,13},{5,1},{9,5},{13,9},{2,14},{6,2},{... | collective-permute-start | bytes 294920 | tf_op jit(solution)/shard_map/ppermute | solution.py:407
  6.2 6.7 %collective-permute-start.2 = (bf16[12,32,128]{2,1,0:T(8,128)(2,1)S(1)}, bf16[12,32,128]{2,1,0:T(8,128)(2,1)S(1)}, u32[]{:S(2)}, u32[]{:S(2)}) collective-permute-start(bf16[12,32,128]{2,1,0:T(8,128)(2,1)S(1)} %get-tuple-element.22), channel_id=1, source_target_pairs={{0,4},{4,8},{8,12},{12,0},{1,5},{5,9},{9,13},{13,1},{2,6},{6,10},{... | collective-permute-start | bytes 294920 | tf_op jit(solution)/shard_map/ppermute | solution.py:407
  13.3 10.1 %collective-permute-start.3 = (bf16[64,768]{1,0:T(8,128)(2,1)S(1)}, bf16[64,768]{1,0:T(8,128)(2,1)S(1)}, u32[]{:S(2)}, u32[]{:S(2)}) collective-permute-start(bf16[64,768]{1,0:T(8,128)(2,1)S(1)} %get-tuple-element.24), channel_id=1, source_target_pairs={{0,4},{4,12},{12,8},{8,0},{1,5},{5,13},{13,9},{9,1},{2,6},{6,14},{... | collective-permute-start | bytes 294920 | tf_op jit(solution)/shard_map/ppermute | solution.py:415
  14.4 9.1 %collective-permute-start.4 = (bf16[64,768]{1,0:T(8,128)(2,1)S(1)}, bf16[64,768]{1,0:T(8,128)(2,1)S(1)}, u32[]{:S(2)}, u32[]{:S(2)}) collective-permute-start(bf16[64,768]{1,0:T(8,128)(2,1)S(1)} %get-tuple-element.25), channel_id=1, source_target_pairs={{0,8},{4,0},{12,4},{8,12},{1,9},{5,1},{13,5},{9,13},{2,10},{6,2},{... | collective-permute-start | bytes 294920 | tf_op jit(solution)/shard_map/ppermute | solution.py:415
  16.7 6.7 %collective-permute-start.5 = (bf16[64,768]{1,0:T(8,128)(2,1)S(1)}, bf16[64,768]{1,0:T(8,128)(2,1)S(1)}, u32[]{:S(2)}, u32[]{:S(2)}) collective-permute-start(bf16[64,768]{1,0:T(8,128)(2,1)S(1)} %get-tuple-element.26), channel_id=1, source_target_pairs={{0,12},{4,8},{12,0},{8,4},{1,13},{5,9},{13,1},{9,5},{2,14},{6,10},... | collective-permute-start | bytes 294920 | tf_op jit(solution)/shard_map/ppermute | solution.py:415

commit v3 on v2

--- a/solution.py
+++ b/solution.py
@@ -185,7 +185,7 @@
 
 
 def ring_place(place):
-    return place ^ (place >> 1)
+    return (place & 1) * 2 + (place >> 1)
 
 
 def table_place(number):
@@ -268,7 +268,7 @@
             if ordered:
                 target = half * (columns // block) + number
                 k = (ring_place(target) - ring_place(z_place) + spaces) % spaces
-                k = jnp.where(k > 1, spaces + 1 - k, k)
+                k = jnp.where(k > 0, spaces - k, k)
                 rotate(spinor, k * moms * 4 * block, 4 * block, block)
             else:
                 rotate(spinor, half * columns, 8 * columns, 2 * columns)
@@ -296,7 +296,7 @@
     columns, plane = weave_ref.shape[1:]
     wide = 4 * columns
     gamma_columns, units = unit_rows(SINGLES[2])
-    step = 16
+    step = columns
 
     def one_colour(c, links, first_row):
         rows = pl.ds(first_row, step)
@@ -409,7 +409,7 @@
 
 def passed_around(value, axis, number):
     count = lax.axis_size(axis)
-    steps = 1 if number == 1 else count + 1 - number
+    steps = count - number
     at = {ring_place(device): device for device in range(count)}
     pairs = [(at[place], at[(place + steps) % count]) for place in range(count)]
     return lax.ppermute(value, axis, pairs)

time: 24.9 us -> 24.5 us (0.984)
  transfers between devices with their start and end apart: 6 -> 6, of which waited for: 3 -> 4; matrix products, arithmetic and copies ran while one was open for 0% -> 0% of each run, Pallas kernels for 12% -> 13%
where the time goes in v3:
time: 24.5 us; the launch traced here: 24.3 us
  waiting for transfers between devices  10.8 us (44%)
  starting transfers between devices  8.81 us (36%)
  Pallas kernels  4.71 us (19%)
    ppermute x3, waiting for transfers between devices, passed_around(): return lax.ppermute(value, axis, pairs)  5.46 us
    ppermute x3, waiting for transfers between devices, passed_along(): return lax.ppermute(value, axis, pairs)  5.32 us
    ppermute x3, starting transfers between devices, passed_along(): return lax.ppermute(value, axis, pairs)  5.14 us
    ppermute x3, starting transfers between devices, passed_around(): return lax.ppermute(value, axis, pairs)  3.67 us
    pallas_call x1, Pallas kernels, body(): call(functools.partial(local_kernel, width=LX, spaces=spaces, ordered=ord...  1.4 us
    pallas_call x1, Pallas kernels, body(): call(functools.partial(insertion_kernel, scaling=scaling), shape((2, moms...  1.21 us
    pallas_call x1, Pallas kernels, body(): call(halo_kernel, [half, half] + [shape(v.shape, v.dtype) for v in (fwd,...  1.04 us
    pallas_call x2, Pallas kernels, more(): return call(kernel, shapes, [VMEM] * 2, 10 ** 9)(left, right)  0.64 us
  transfers between devices with their start and end apart: 6, of which 4 were waited for; matrix products, arithmetic and copies ran while one was open for 0% of the time, Pallas kernels for 13%

profile of v3, /device:TPU:0, one launch (start us, length us, event | category | flops | bytes accessed | tf_op | source)
XLA Modules:
  0.0 24.3 jit_solution(5968054000190890644)
XLA Ops:
  0.0 0.5 %collective-permute-start = (bf16[24,32,128]{2,1,0:T(8,128)(2,1)}, bf16[24,32,128]{2,1,0:T(8,128)(2,1)S(1)}, u32[]{:S(2)}, u32[]{:S(2)}) collective-permute-start(bf16[24,32,128]{2,1,0:T(8,128)(2,1)} %bitcast.21), channel_id=1, source_target_pairs={{0,1},{1,0},{2,3},{3,2},{4,5},{5,4},{6,7},{7,6},{8,9},{9,8},{10,11... | collective-permute-start | bytes 589832 | tf_op jit(solution)/shard_map/ppermute | solution.py:407
  0.5 1.0 %shard_map.55 = (bf16[12,32,128]{2,1,0:T(8,128)(2,1)S(1)}, bf16[12,32,128]{2,1,0:T(8,128)(2,1)S(1)}, bf16[24,32,128]{2,1,0:T(8,128)(2,1)S(1)}, bf16[27,2,128]{2,1,0:T(2,128)(2,1)S(1)}) custom-call(bf16[24,32,128]{2,1,0:T(8,128)(2,1)} %bitcast.20, bf16[27,2,128]{2,1,0:T(2,128)(2,1)} %bitcast.23), custom_call_target="tpu_custom_call" | custom-call | flops 10000000 | bytes 1048576 | tf_op jit(solution)/shard_map/pallas_call | solution.py:453
  1.5 4.6 %collective-permute-start.1 = (bf16[12,32,128]{2,1,0:T(8,128)(2,1)S(1)}, bf16[12,32,128]{2,1,0:T(8,128)(2,1)S(1)}, u32[]{:S(2)}, u32[]{:S(2)}) collective-permute-start(bf16[12,32,128]{2,1,0:T(8,128)(2,1)S(1)} %get-tuple-element.21), channel_id=1, source_target_pairs={{0,12},{4,0},{8,4},{12,8},{1,13},{5,1},{9,5},{13,9},{2,14},{6,2},{... | collective-permute-start | bytes 294920 | tf_op jit(solution)/shard_map/ppermute | solution.py:407
  6.2 0.0 collective-permute-start.2
  6.2 0.0 collective-permute-done.other_ref
  6.2 1.4 %shard_map.56 = (f32[24,32,128]{2,1,0:T(8,128)S(1)}, bf16[768,768]{1,0:T(8,128)(2,1)S(1)}, s32[16,128]{1,0:T(8,128)S(1)}) custom-call(s32[3,3]{1,0:T(4,128)} %momenta_hbm.1, bf16[24,32,128]{2,1,0:T(8,128)(2,1)} %bitcast.22, s32[16]{0:T(128)} %list_hbm.1, bf16[24,32,128]{2,1,0:T(8,128)(2,1)S(1)} %get-tuple-element.16.fwd_ref, ...), custom_call_target="tpu_custom_call" | custom-call | flops 100000000 | bytes 1048576 | tf_op jit(solution)/shard_map/pallas_call | solution.py:463
  7.6 1.8 %collective-permute-done.1.ahead_ref = bf16[12,32,128]{2,1,0:T(8,128)(2,1)S(1)} collective-permute-done((bf16[12,32,128]{2,1,0:T(8,128)(2,1)S(1)}, bf16[12,32,128]{2,1,0:T(8,128)(2,1)S(1)}, u32[]{:S(2)}, u32[]{:S(2)}) %collective-permute-start.1) | collective-permute-done | bytes 98336 | tf_op jit(solution)/shard_map/ppermute | solution.py:407
  9.4 3.5 %collective-permute-done.2.behind_ref = bf16[12,32,128]{2,1,0:T(8,128)(2,1)S(1)} collective-permute-done((bf16[12,32,128]{2,1,0:T(8,128)(2,1)S(1)}, bf16[12,32,128]{2,1,0:T(8,128)(2,1)S(1)}, u32[]{:S(2)}, u32[]{:S(2)}) %collective-permute-start.2) | collective-permute-done | bytes 98336 | tf_op jit(solution)/shard_map/ppermute | solution.py:407
  12.9 0.4 %shard_map.57 = (bf16[256,768]{1,0:T(8,128)(2,1)S(1)}, bf16[64,768]{1,0:T(8,128)(2,1)S(1)}) custom-call(f32[24,32,128]{2,1,0:T(8,128)S(1)} %get-tuple-element.20.weave_ref, bf16[12,32,128]{2,1,0:T(8,128)(2,1)S(1)} %collective-permute-done.1.ahead_ref, bf16[12,32,128]{2,1,0:T(8,128)(2,1)S(1)} %collective-permute-done.2.behind_ref, ...), custom_call_target="tpu_custom_call" | custom-call | flops 1000000000 | bytes 1048576 | tf_op jit(solution)/shard_map/pallas_call | solution.py:483
  13.3 0.8 %collective-permute-start.3 = (bf16[64,768]{1,0:T(8,128)(2,1)S(1)}, bf16[64,768]{1,0:T(8,128)(2,1)S(1)}, u32[]{:S(2)}, u32[]{:S(2)}) collective-permute-start(bf16[64,768]{1,0:T(8,128)(2,1)S(1)} %get-tuple-element.24), channel_id=1, source_target_pairs={{0,12},{8,0},{4,8},{12,4},{1,13},{9,1},{5,9},{13,5},{2,14},{10,2},... | collective-permute-start | bytes 294920 | tf_op jit(solution)/shard_map/ppermute | solution.py:415
  14.2 0.3 %shard_map.59 = (bf16[64,768]{1,0:T(8,128)(2,1)S(1)}, bf16[64,768]{1,0:T(8,128)(2,1)S(1)}) custom-call(bf16[768,768]{1,0:T(8,128)(2,1)S(1)} %get-tuple-element.19.left_ref, bf16[256,768]{1,0:T(8,128)(2,1)S(1)} %get-tuple-element.23.right_ref), custom_call_target="tpu_custom_call" | custom-call | flops 1000000000 | bytes 1048576 | tf_op jit(solution)/shard_map/pallas_call | solution.py:493
  14.5 0.1 collective-permute-start.4
  14.6 2.8 %collective-permute-start.5 = (bf16[64,768]{1,0:T(8,128)(2,1)S(1)}, bf16[64,768]{1,0:T(8,128)(2,1)S(1)}, u32[]{:S(2)}, u32[]{:S(2)}) collective-permute-start(bf16[64,768]{1,0:T(8,128)(2,1)S(1)} %get-tuple-element.26), channel_id=1, source_target_pairs={{0,8},{8,4},{4,12},{12,0},{1,9},{9,5},{5,13},{13,1},{2,10},{10,6},... | collective-permute-start | bytes 294920 | tf_op jit(solution)/shard_map/ppermute | solution.py:415
  17.4 0.3 %shard_map.58 = f32[64,768]{1,0:T(8,128)S(1)} custom-call(bf16[768,768]{1,0:T(8,128)(2,1)S(1)} %get-tuple-element.19.left_ref, bf16[256,768]{1,0:T(8,128)(2,1)S(1)} %get-tuple-element.23.right_ref), custom_call_target="tpu_custom_call" | custom-call | flops 1000000000 | bytes 1048576 | tf_op jit(solution)/shard_map/pallas_call | solution.py:493
  17.7 4.4 %collective-permute-done.3 = bf16[64,768]{1,0:T(8,128)(2,1)S(1)} collective-permute-done((bf16[64,768]{1,0:T(8,128)(2,1)S(1)}, bf16[64,768]{1,0:T(8,128)(2,1)S(1)}, u32[]{:S(2)}, u32[]{:S(2)}) %collective-permute-start.3) | collective-permute-done | bytes 98336 | tf_op jit(solution)/shard_map/ppermute | solution.py:415
  22.1 0.0 collective-permute-done.4
  22.1 1.1 %collective-permute-done.5 = bf16[64,768]{1,0:T(8,128)(2,1)S(1)} collective-permute-done((bf16[64,768]{1,0:T(8,128)(2,1)S(1)}, bf16[64,768]{1,0:T(8,128)(2,1)S(1)}, u32[]{:S(2)}, u32[]{:S(2)}) %collective-permute-start.5) | collective-permute-done | bytes 98336 | tf_op jit(solution)/shard_map/ppermute | solution.py:415
  23.1 1.2 %shard_map.60 = f32[2,3,16,16,32]{4,3,2,1,0:T(8,128)} custom-call(s32[16,128]{1,0:T(8,128)S(1)} %get-tuple-element.18.places_ref, f32[1,64,768]{2,1,0:T(8,128)S(1)} %bitcast.16, bf16[1,64,768]{2,1,0:T(8,128)(2,1)S(1)} %bitcast.17, bf16[1,64,768]{2,1,0:T(8,128)(2,1)S(1)} %bitcast.18, bf16[1,64,768]{2,1,0:T(8,128)(2,1)S(1)} %bitcast.19), custom_call_target="tpu_custom_call" | custom-call | flops 100000000 | bytes 1048576 | tf_op jit(solution)/shard_map/pallas_call | solution.py:507
Async XLA Ops:
  0.0 6.2 %collective-permute-start = (bf16[24,32,128]{2,1,0:T(8,128)(2,1)}, bf16[24,32,128]{2,1,0:T(8,128)(2,1)S(1)}, u32[]{:S(2)}, u32[]{:S(2)}) collective-permute-start(bf16[24,32,128]{2,1,0:T(8,128)(2,1)} %bitcast.21), channel_id=1, source_target_pairs={{0,1},{1,0},{2,3},{3,2},{4,5},{5,4},{6,7},{7,6},{8,9},{9,8},{10,11... | collective-permute-start | bytes 589832 | tf_op jit(solution)/shard_map/ppermute | solution.py:407
  1.5 7.9 %collective-permute-start.1 = (bf16[12,32,128]{2,1,0:T(8,128)(2,1)S(1)}, bf16[12,32,128]{2,1,0:T(8,128)(2,1)S(1)}, u32[]{:S(2)}, u32[]{:S(2)}) collective-permute-start(bf16[12,32,128]{2,1,0:T(8,128)(2,1)S(1)} %get-tuple-element.21), channel_id=1, source_target_pairs={{0,12},{4,0},{8,4},{12,8},{1,13},{5,1},{9,5},{13,9},{2,14},{6,2},{... | collective-permute-start | bytes 294920 | tf_op jit(solution)/shard_map/ppermute | solution.py:407
  6.2 6.7 %collective-permute-start.2 = (bf16[12,32,128]{2,1,0:T(8,128)(2,1)S(1)}, bf16[12,32,128]{2,1,0:T(8,128)(2,1)S(1)}, u32[]{:S(2)}, u32[]{:S(2)}) collective-permute-start(bf16[12,32,128]{2,1,0:T(8,128)(2,1)S(1)} %get-tuple-element.22), channel_id=1, source_target_pairs={{0,4},{4,8},{8,12},{12,0},{1,5},{5,9},{9,13},{13,1},{2,6},{6,10},{... | collective-permute-start | bytes 294920 | tf_op jit(solution)/shard_map/ppermute | solution.py:407
  13.3 8.7 %collective-permute-start.3 = (bf16[64,768]{1,0:T(8,128)(2,1)S(1)}, bf16[64,768]{1,0:T(8,128)(2,1)S(1)}, u32[]{:S(2)}, u32[]{:S(2)}) collective-permute-start(bf16[64,768]{1,0:T(8,128)(2,1)S(1)} %get-tuple-element.24), channel_id=1, source_target_pairs={{0,12},{8,0},{4,8},{12,4},{1,13},{9,1},{5,9},{13,5},{2,14},{10,2},... | collective-permute-start | bytes 294920 | tf_op jit(solution)/shard_map/ppermute | solution.py:415
  14.5 7.5 %collective-permute-start.4 = (bf16[64,768]{1,0:T(8,128)(2,1)S(1)}, bf16[64,768]{1,0:T(8,128)(2,1)S(1)}, u32[]{:S(2)}, u32[]{:S(2)}) collective-permute-start(bf16[64,768]{1,0:T(8,128)(2,1)S(1)} %get-tuple-element.25), channel_id=1, source_target_pairs={{0,4},{8,12},{4,0},{12,8},{1,5},{9,13},{5,1},{13,9},{2,6},{10,14},... | collective-permute-start | bytes 294920 | tf_op jit(solution)/shard_map/ppermute | solution.py:415
  14.6 8.5 %collective-permute-start.5 = (bf16[64,768]{1,0:T(8,128)(2,1)S(1)}, bf16[64,768]{1,0:T(8,128)(2,1)S(1)}, u32[]{:S(2)}, u32[]{:S(2)}) collective-permute-start(bf16[64,768]{1,0:T(8,128)(2,1)S(1)} %get-tuple-element.26), channel_id=1, source_target_pairs={{0,8},{8,4},{4,12},{12,0},{1,9},{9,5},{5,13},{13,1},{2,10},{10,6},... | collective-permute-start | bytes 294920 | tf_op jit(solution)/shard_map/ppermute | solution.py:415
